TPU v7x, 32 devices: a whole 2x2x4 slice. The times are simulated.
32 devices in a mesh: grp: 2 (over y), pulse: 4 (over z), chan: 2 (over x), sub: 2 (over core).
Axes of the slice: x: 2, y: 2, z: 4, core: 2. Of those that a mesh axis runs over, the one named last changes fastest.
Arguments:
- samples: int32 [2, 16, 512, 4096], P(None, ('grp', 'chan', 'sub'), 'pulse'), parts along dimension 1, may hold values from -2048 to 2047
- replica: float32 [2, 4096], replicated, may hold values from -6 to 6
- window: int32 [16, 2], P(('grp', 'chan', 'sub')), parts along dimension 0, may hold values from 1 to 28, as said below
- thresh: int32 [16, 2], P(('grp', 'chan', 'sub')), parts along dimension 0, may hold values from 2 to 32, as said below
Outputs:
- ratio_map: float32 [16, 512, 4096], P(('grp', 'chan', 'sub'), None, 'pulse'), parts along dimension 0
- detections: float32 [2], P('grp'), parts along dimension 0
There are 2 independent parts, one for each index of `grp`. A program takes and returns all parts, laid end to end along the dimension named above; an argument that names none is the same for every part. Nothing has to cross between parts.
Inputs may be any that keep to these rules, and one draw needn't show every extreme that they name: `window`: column 0 is a channel's guard gates on each side, 1 to 4; column 1 its training gates on each side, 14 to 28; some channel has both at their most. `thresh`: column 0 is a numerator of 8 to 32, column 1 a denominator of 2 to 4.
All inputs are finite; a program needn't handle non-finite values.
Results may differ from a plain program's by a relative error of at most 0.0003.
Values sent between devices are 32-bit elements; how exact they have to be, the bound alone decides.
A program may use at most 128 MiB of HBM per device.

v0:
```python
import math

import jax
import jax.numpy as jnp
from jax import lax
from jax.sharding import PartitionSpec as P

PULSES = 512
RANGE = 4096
GUARD_MAX = 4
TRAIN_MAX = 28


HIGHEST = lax.Precision.HIGHEST
EPSILON = 1e-06
INPUT_SCALE = 1.0 / 2048.0


def padded_2(cells, sides, width):
    for axis, dim in sides:
        count = lax.axis_size(axis)
        ends = count - 1
        head = lax.slice_in_dim(cells, 0, width, axis=dim)
        tail = lax.slice_in_dim(cells, cells.shape[dim] - width, cells.shape[dim], axis=dim)
        cells = jnp.concatenate(
            [
                lax.ppermute(tail, axis, [(i, (i + 1) % count) for i in range(ends)]),
                cells,
                lax.ppermute(head, axis, [((i + 1) % count, i) for i in range(ends)]),
            ],
            axis=dim,
        )
    return cells


def split_factor(length):
    leading = 1
    for divisor in range(1, math.isqrt(length) + 1):
        if length % divisor == 0:
            leading = divisor
    return (leading, length // leading)


def make_table(rows_n, cols_n, period, sign_val):
    prod_idx = (
        jnp.arange(rows_n, dtype=jnp.int32)[:, None]
        * jnp.arange(cols_n, dtype=jnp.int32)[None, :]
        % period
    )
    angles = 2.0 * math.pi / period * prod_idx.astype(jnp.float32)
    return (jnp.cos(angles), sign_val * jnp.sin(angles))


def dft_tables(lead_len, tail_len, inverse):
    sign_val = 1.0 if inverse else -1.0
    whole_len = lead_len * tail_len
    return (
        make_table(lead_len, lead_len, lead_len, sign_val),
        make_table(lead_len, tail_len, whole_len, sign_val),
        make_table(tail_len, tail_len, tail_len, sign_val),
    )


def complex_einsum(form, x_re, x_im, tables):
    t_re, t_im = tables
    out_re = jnp.einsum(form, x_re, t_re, precision=HIGHEST) - jnp.einsum(
        form, x_im, t_im, precision=HIGHEST
    )
    out_im = jnp.einsum(form, x_re, t_im, precision=HIGHEST) + jnp.einsum(
        form, x_im, t_re, precision=HIGHEST
    )
    return (out_re, out_im)


def transform_last(x_re, x_im, inverse):
    length = x_re.shape[-1]
    lead_len, tail_len = split_factor(length)
    first_section, twiddle, second_section = dft_tables(lead_len, tail_len, inverse)
    split_shape = x_re.shape[:-1] + (lead_len, tail_len)
    mid_re, mid_im = complex_einsum(
        "...ab,ak->...kb", x_re.reshape(split_shape), x_im.reshape(split_shape), first_section
    )
    tw_re, tw_im = twiddle
    mid_re, mid_im = (mid_re * tw_re - mid_im * tw_im, mid_re * tw_im + mid_im * tw_re)
    end_re, end_im = complex_einsum("...kb,bm->...mk", mid_re, mid_im, second_section)
    factor = 1.0 / math.sqrt(length)
    return (end_re.reshape(x_re.shape) * factor, end_im.reshape(x_re.shape) * factor)


def transform_cols(x_re, x_im):
    length = x_re.shape[-2]
    lead_len, tail_len = split_factor(length)
    first_section, twiddle, second_section = dft_tables(lead_len, tail_len, False)
    split_shape = x_re.shape[:-2] + (lead_len, tail_len, x_re.shape[-1])
    mid_re, mid_im = complex_einsum(
        "...abl,ak->...kbl", x_re.reshape(split_shape), x_im.reshape(split_shape), first_section
    )
    tw_re = twiddle[0][:, :, None]
    tw_im = twiddle[1][:, :, None]
    mid_re, mid_im = (mid_re * tw_re - mid_im * tw_im, mid_re * tw_im + mid_im * tw_re)
    end_re, end_im = complex_einsum("...kbl,bm->...mkl", mid_re, mid_im, second_section)
    factor = 1.0 / math.sqrt(length)
    return (end_re.reshape(x_re.shape) * factor, end_im.reshape(x_re.shape) * factor)


def doppler_power(turned):
    dop_re, dop_im = transform_cols(turned[0], turned[1])
    return dop_re * dop_re + dop_im * dop_im


def local(samples, replica, window, thresh):
    margin = GUARD_MAX + TRAIN_MAX
    groups = lax.axis_size("pulse")
    spec_re = replica[0]
    spec_im = replica[1]
    pieces_list = []
    for channel in range(samples.shape[1]):
        chan_block = samples[:, channel : channel + 1]
        sig_re = chan_block[0].astype(jnp.float32) * INPUT_SCALE
        sig_im = chan_block[1].astype(jnp.float32) * INPUT_SCALE
        freq_re, freq_im = transform_last(sig_re, sig_im, False)
        prod_re = freq_re * spec_re - freq_im * spec_im
        prod_im = freq_re * spec_im + freq_im * spec_re
        comp_re, comp_im = transform_last(prod_re, prod_im, True)
        stacked = jnp.stack([comp_re, comp_im])
        pieces_list.append(
            doppler_power(lax.all_to_all(stacked, "pulse", split_axis=3, concat_axis=2, tiled=True))
        )
    power = jnp.concatenate(pieces_list, axis=0)
    padded = padded_2(power, (("pulse", 2),), margin)
    gates = padded.shape[2] - 2 * margin
    span = gates + 2 * margin
    rel_pos = (
        jnp.arange(span, dtype=jnp.int32)[:, None]
        - margin
        - jnp.arange(gates, dtype=jnp.int32)[None, :]
    )
    distance = jnp.abs(rel_pos)[None]
    guard = window[:, 0][:, None, None]
    train = window[:, 1][:, None, None]
    band = ((distance > guard) & (distance <= guard + train)).astype(jnp.float32)
    global_pos = lax.axis_index("pulse") * gates + jnp.arange(span, dtype=jnp.int32) - margin
    inside = ((global_pos >= 0) & (global_pos < gates * groups)).astype(jnp.float32)
    cells = jnp.einsum("cjr,j->cr", band, inside, precision=HIGHEST)
    noise_sum = jnp.einsum("cdj,cjr->cdr", padded, band, precision=HIGHEST)
    core = padded[:, :, margin : margin + gates]
    level = (noise_sum + EPSILON) / cells[:, None, :]
    ratio_map = core / level
    scale = thresh[:, 0].astype(jnp.float32) / thresh[:, 1].astype(jnp.float32)
    soft = jnp.clip(ratio_map / scale[:, None, None] - 1.0, 0.0, 1.0)
    partial_sum = jnp.sum(soft) * (1024.0 / (PULSES * RANGE))
    detections = lax.psum(partial_sum, ("pulse", "chan", "sub"))
    return (ratio_map, detections.reshape(1))


def solution(mesh):
    in_specs = (
        P(None, ("grp", "chan", "sub"), "pulse", None),
        P(),
        P(("grp", "chan", "sub"), None),
        P(("grp", "chan", "sub"), None),
    )
    out_specs = (P(("grp", "chan", "sub"), None, "pulse"), P("grp"))
    return jax.shard_map(local, mesh=mesh, in_specs=in_specs, out_specs=out_specs, check_vma=False)
```

profile of v0, /device:TPU:0, one launch (start us, length us, event | category | flops | bytes accessed | tf_op | source)
XLA Modules:
  0.0 493.2 jit_solution(2112341081693169330)
XLA Ops:
  0.6 7.1 %fusion.571 = (s32[1,1,128,4096]{3,2,1,0:T(8,128)}, s32[1,1,128,4096]{3,2,1,0:T(8,128)}, s32[1,1,128,4096]{3,2,1,0:T(8,128)}, s32[1,1,128,4096]{3,2,1,0:T(8,128)}) fusion(s32[2,2,128,4096]{3,2,1,0:T(8,128)} %param.4), kind=kLoop, calls=%fused_computation.547 | loop fusion | bytes 16777216 | tf_op jit(solution)/shard_map/slice | solution.py:119
  9.8 4.5 fusion.126
  14.2 4.4 fusion.124
  24.0 4.4 fusion.86
  34.2 4.5 fusion.132
  38.7 4.5 fusion.135
  51.1 6.2 %fusion.31 = (f32[128,64,64]{0,1,2:T(8,128)S(1)}, f32[128,64,64]{0,1,2:T(8,128)S(1)}, f32[128,64,64]{0,1,2:T(8,128)S(1)}, f32[128,64,64]{0,1,2:T(8,128)}) fusion(f32[64,128,64]{1,0,2:T(8,128)S(1)} %fusion.159, f32[64,64]{0,1:T(8,128)S(1)} %get-tuple-element.44, f32[64,64]{0,1:T(8,128)S(1)} %get-tuple-element.45, f32[64,128,64]{1,0,2:T(8,128)S(1)} %copy-done.4, ...), kind=kOutput, calls=%fused_computation.52 | convolution fusion | flops 409526272 | bytes 18907136 | tf_op jit(solution)/shard_map/...ab,ak->...kb/dot_general | solution.py:66
  57.3 4.4 fusion.78
  61.8 4.4 fusion.76
  66.2 4.5 fusion.118
  70.7 4.7 fusion.116
  75.7 5.5 %fusion.138 = f32[64,128,64]{1,0,2:T(8,128)S(1)} fusion(f32[64,128,64]{1,0,2:T(8,128)} %fusion.118, f32[128,64,64]{0,1,2:T(8,128)} %get-tuple-element.41), kind=kOutput, calls=%fused_computation.183 | convolution fusion | flops 403234816 | bytes 6291456 | tf_op jit(solution)/shard_map/...kb,bm->...mk/dot_general | solution.py:66
  111.6 5.4 %fusion.17 = (f32[128,64,64]{0,1,2:T(8,128)S(1)}, f32[128,64,64]{0,1,2:T(8,128)}, f32[128,64,64]{0,1,2:T(8,128)S(1)}, f32[128,64,64]{0,1,2:T(8,128)S(1)}) fusion(f32[64,128,64]{1,0,2:T(8,128)S(1)} %fusion.186, f32[64,64]{0,1:T(8,128)S(1)} %fusion.277, f32[64,64]{0,1:T(8,128)S(1)} %get-tuple-element.45, f32[64,128,64]{1,0,2:T(8,128)S(1)} %fusion.183, ...), kind=kOutput, calls=%fused_computation.30 | convolution fusion | flops 411099136 | bytes 21037056 | tf_op jit(solution)/shard_map/...ab,ak->...kb/dot_general | solution.py:69
  132.6 19.2 %copy.168 = f32[2,1,128,4096]{2,1,0,3:T(1,128)} copy(f32[2,1,128,4096]{2,3,1,0:T(8,128)S(1)} %pad_maximum_fusion.1) | data formatting | bytes 8388608 | tf_op jit(solution)/shard_map/stack | solution.py:125
  151.8 6.3 %all-to-all-start = ((f32[2,1,128,4096]{2,1,0,3:T(1,128)}), f32[2,1,128,4096]{2,1,0,3:T(1,128)}, u32[]{:S(2)}, u32[]{:S(2)}) async-start(f32[2,1,128,4096]{2,1,0,3:T(1,128)} %copy.168), calls=%async_computation | async-start | bytes 8388608 | tf_op jit(solution)/shard_map/all_to_all | solution.py:127
  158.1 4.7 fusion.70
  175.9 19.2 %copy.197 = f32[2,1,128,4096]{2,1,0,3:T(1,128)} copy(f32[2,1,128,4096]{2,3,1,0:T(8,128)S(1)} %pad_maximum_fusion.2) | data formatting | bytes 8388608 | tf_op jit(solution)/shard_map/stack | solution.py:125
  195.0 56.5 %all-to-all-done = f32[2,1,128,4096]{2,1,0,3:T(1,128)} async-done(((f32[2,1,128,4096]{2,1,0,3:T(1,128)}), f32[2,1,128,4096]{2,1,0,3:T(1,128)}, u32[]{:S(2)}, u32[]{:S(2)}) %all-to-all-start) | async-done | bytes 4194336 | tf_op jit(solution)/shard_map/all_to_all | solution.py:127
  251.5 4.9 all-to-all-start.1
  274.6 74.5 %all-to-all-done.1 = f32[2,1,128,4096]{2,1,0,3:T(1,128)} async-done(((f32[2,1,128,4096]{2,1,0,3:T(1,128)}), f32[2,1,128,4096]{2,1,0,3:T(1,128)}, u32[]{:S(2)}, u32[]{:S(2)}) %all-to-all-start.1) | async-done | bytes 4194336 | tf_op jit(solution)/shard_map/all_to_all | solution.py:127
  356.0 4.3 fusion.62
  360.2 4.2 fusion.60
  366.6 5.9 %fusion.148 = f32[16,32,1024]{2,0,1:T(8,128)} fusion(f32[16,32,1024]{2,0,1:T(8,128)} %fusion.102, f32[16,32,1024]{2,1,0:T(8,128)S(1)} %bitcast.378), kind=kOutput, calls=%fused_computation.185 | convolution fusion | flops 101191168 | bytes 6291456 | tf_op jit(solution)/shard_map/...abl,ak->...kbl/dot_general | solution.py:66
  372.5 4.3 fusion.151
  378.8 5.3 %fusion.172 = f32[16,32,1024]{2,0,1:T(8,128)S(1)} fusion(f32[16,32,1024]{2,0,1:T(8,128)} %fusion.62, f32[16,32,1024]{2,1,0:T(8,128)S(1)} %bitcast.372), kind=kOutput, calls=%fused_computation.191 | convolution fusion | flops 101191168 | bytes 6291456 | tf_op jit(solution)/shard_map/...abl,ak->...kbl/dot_general | solution.py:66
  384.2 6.0 %multiply_add_fusion.1 = (f32[16,32,1024]{2,0,1:T(8,128)S(1)}, f32[16,32,1024]{2,0,1:T(8,128)S(1)}, f32[16,32,1024]{2,0,1:T(8,128)S(1)}, f32[16,32,1024]{2,0,1:T(8,128)S(1)}) fusion(f32[16,32,1024]{2,0,1:T(8,128)S(1)} %fusion.172, f32[16,32]{0,1:T(8,128)S(1)} %get-tuple-element.46, f32[16,32]{0,1:T(8,128)S(1)} %get-tuple-element.47, ...), kind=kOutput, calls=%fused_computation.88 | convolution fusion | flops 107482880 | bytes 18878464 | tf_op jit(solution)/shard_map/...abl,ak->...kbl/dot_general | solution.py:69
  396.2 4.3 fusion.52
  400.5 4.4 fusion.54
  433.5 4.3 fusion.1
  438.8 15.0 %clamp_reduce_fusion = (f32[]{:T(128)}, f32[2,512,1024]{1,2,0:T(8,128)}) fusion(f32[1,512,1024]{1,2,0:T(8,128)S(1)} %copy-done.18, f32[1,512,1024]{1,2,0:T(8,128)S(1)} %copy-done.17, f32[2]{0:T(128)S(1)} %fusion.361, f32[2,1024]{1,0:T(2,128)S(1)} %bitcast.396, s32[1088,1024]{1,0:T(8,128)} %subtract_abs_fusion, s32[2]{0:T(128)S(1)} %add.422, ...), kind=kOutput, calls=%fused_computation.25 | convolution fusion | flops 13709672448 | bytes 13115420 | tf_op jit(solution)/shard_map/cdj,cjr->cdr/dot_general | solution.py:145
  453.8 5.3 %copy.213 = f32[2,512,1024]{2,1,0:T(8,128)} copy(f32[2,512,1024]{1,2,0:T(8,128)} %get-tuple-element.15) | data formatting | bytes 8388608
  459.8 32.9 %psum.7 = f32[1]{0:T(128)} all-reduce(f32[1]{0:T(128)} %bitcast.84), channel_id=1, replica_groups=mesh['grp'=2,'pulse'=4,'chan'=2,'sub'=2] {'pulse','chan','sub'}, use_global_device_ids=true, to_apply=%region_1.2 | all-reduce | flops 1 | bytes 8 | tf_op jit(solution)/shard_map/psum | solution.py:152
  (118 shorter events, 144.8 us)
Async XLA Ops:
  31.9 2.2 copy-start.13
  34.2 4.5 copy-start.12
  47.9 3.2 copy-start.3
  47.9 3.2 copy-start.4
  47.9 3.2 copy-start.8
  70.7 4.7 copy-start.19
  75.7 5.5 %copy-start = (f32[128,64,64]{0,1,2:T(8,128)S(1)}, f32[128,64,64]{0,1,2:T(8,128)}, u32[]{:S(2)}) copy-start(f32[128,64,64]{0,1,2:T(8,128)} %get-tuple-element.41) | copy-start | bytes 6291460
  75.7 5.5 %copy-start.14 = (f32[64,128,64]{1,0,2:T(8,128)S(1)}, f32[64,128,64]{1,0,2:T(8,128)}, u32[]{:S(2)}) copy-start(f32[64,128,64]{1,0,2:T(8,128)} %fusion.116) | copy-start | bytes 6291460
  87.2 2.9 copy-start.9
  90.1 3.6 copy-start.7
  151.8 99.8 %all-to-all-start = ((f32[2,1,128,4096]{2,1,0,3:T(1,128)}), f32[2,1,128,4096]{2,1,0,3:T(1,128)}, u32[]{:S(2)}, u32[]{:S(2)}) async-start(f32[2,1,128,4096]{2,1,0,3:T(1,128)} %copy.168), calls=%async_computation | async-start | bytes 8388608 | tf_op jit(solution)/shard_map/all_to_all | solution.py:127
  166.0 1.6 copy-start.2
  195.0 61.4 %copy-start.21 = (s32[2,2]{1,0:T(2,128)S(1)}, s32[2,2]{1,0:T(2,128)}, u32[]{:S(2)}) copy-start(s32[2,2]{1,0:T(2,128)} %param.6) | copy-start | bytes 52
  251.5 97.5 %all-to-all-start.1 = ((f32[2,1,128,4096]{2,1,0,3:T(1,128)}), f32[2,1,128,4096]{2,1,0,3:T(1,128)}, u32[]{:S(2)}, u32[]{:S(2)}) async-start(f32[2,1,128,4096]{2,1,0,3:T(1,128)} %copy.197), calls=%async_computation.1 | async-start | bytes 8388608 | tf_op jit(solution)/shard_map/all_to_all | solution.py:127
  366.6 5.9 %copy-start.10 = (f32[16,32,1024]{2,0,1:T(8,128)S(1)}, f32[16,32,1024]{2,0,1:T(8,128)}, u32[]{:S(2)}) copy-start(f32[16,32,1024]{2,0,1:T(8,128)} %fusion.100) | copy-start | bytes 6291460
  378.7 5.4 %copy-start.1 = (f32[1,1,4,128,1024]{4,3,2,1,0:T(8,128)}, f32[1,1,4,128,1024]{4,3,2,1,0:T(8,128)S(1)}, u32[]{:S(2)}) copy-start(f32[1,1,4,128,1024]{4,3,2,1,0:T(8,128)S(1)} %copy.199) | copy-start | bytes 6291460
  378.8 5.4 %copy-start.5 = (f32[16,32,1024]{2,0,1:T(8,128)S(1)}, f32[16,32,1024]{2,0,1:T(8,128)}, u32[]{:S(2)}) copy-start(f32[16,32,1024]{2,0,1:T(8,128)} %fusion.148) | copy-start | bytes 6291460
  378.8 5.4 %copy-start.6 = (f32[16,32,1024]{2,0,1:T(8,128)S(1)}, f32[16,32,1024]{2,0,1:T(8,128)}, u32[]{:S(2)}) copy-start(f32[16,32,1024]{2,0,1:T(8,128)} %fusion.151) | copy-start | bytes 6291460
  378.8 5.4 %copy-start.11 = (f32[16,32,1024]{2,0,1:T(8,128)S(1)}, f32[16,32,1024]{2,0,1:T(8,128)}, u32[]{:S(2)}) copy-start(f32[16,32,1024]{2,0,1:T(8,128)} %fusion.60) | copy-start | bytes 6291460
  417.4 3.1 copy-start.15
  417.4 3.1 copy-start.16
  426.5 3.1 copy-start.17
  430.5 7.5 %collective-permute-start = (f32[2,512,32]{1,2,0:T(8,128)S(1)}, f32[2,512,32]{1,2,0:T(8,128)S(1)}, u32[]{:S(2)}, u32[]{:S(2)}) collective-permute-start(f32[2,512,32]{1,2,0:T(8,128)S(1)} %get-tuple-element.32), channel_id=1, source_target_pairs={{0,4},{4,8},{8,12},{1,5},{5,9},{9,13},{2,6},{6,10},{10,14},{3,7},{... | collective-permute-start | bytes 393224 | tf_op jit(solution)/shard_map/ppermute | solution.py:27
  431.8 6.0 %copy-start.20 = (s32[2,2]{1,0:T(2,128)S(1)}, s32[2,2]{1,0:T(2,128)}, u32[]{:S(2)}) copy-start(s32[2,2]{1,0:T(2,128)} %param.7) | copy-start | bytes 52
  431.8 7.0 %copy-start.18 = (f32[1,512,1024]{1,2,0:T(8,128)S(1)}, f32[1,512,1024]{1,2,0:T(8,128)}, u32[]{:S(2)}) copy-start(f32[1,512,1024]{1,2,0:T(8,128)} %copy.211) | copy-start | bytes 6291460
  431.8 7.0 %collective-permute-start.1 = (f32[2,512,32]{1,2,0:T(8,128)S(1)}, f32[2,512,32]{1,2,0:T(8,128)S(1)}, u32[]{:S(2)}, u32[]{:S(2)}) collective-permute-start(f32[2,512,32]{1,2,0:T(8,128)S(1)} %get-tuple-element.33), channel_id=1, source_target_pairs={{4,0},{8,4},{12,8},{5,1},{9,5},{13,9},{6,2},{10,6},{14,10},{7,3},{... | collective-permute-start | bytes 393224 | tf_op jit(solution)/shard_map/ppermute | solution.py:29
where the time goes:
time: 500 us; the launch traced here: 493 us
  matrix products  207 us (41%)
  waiting for transfers between devices  132 us (26%)
  local copies, waits for them, and re-layouts  96.2 us (19%)
  blocking collectives  32.9 us (7%)
  starting transfers between devices  14.2 us (3%)
  other arithmetic  8.68 us (2%)
    all_to_all x2, waiting for transfers between devices, local(): lax.all_to_all(stacked, 'pulse', split_axis=3, concat_axis=2, tiled=True)  131 us
    dot_general x12, matrix products, complex_einsum(): jnp.einsum(form, x_re, t_re, precision=HIGHEST)  50.4 us
    dot_general x12, matrix products, complex_einsum(): jnp.einsum(form, x_im, t_im, precision=HIGHEST)  47.1 us
    dot_general x12, matrix products, complex_einsum(): jnp.einsum(form, x_re, t_im, precision=HIGHEST)  45.8 us
    dot_general x12, matrix products, complex_einsum(): jnp.einsum(form, x_im, t_re, precision=HIGHEST)  44.3 us
    another operation x2, local copies, waits for them, and re-layouts, local(): stacked = jnp.stack([comp_re, comp_im])  38.3 us
    psum x1, blocking collectives, local(): detections = lax.psum(partial_sum, ('pulse', 'chan', 'sub'))  32.9 us
    unnamed x49, local copies, waits for them, and re-layouts  16.4 us
  transfers between devices with their start and end apart: 4, of which 3 were waited for; matrix products, arithmetic and copies ran while one was open for 12% of the time, Pallas kernels for 0%

commit v1 on v0

v1 whole, which is shorter than its diff:
```python
import functools
import math

import jax
import jax.numpy as jnp
import numpy as np
from jax import lax
from jax.experimental import pallas as pl
from jax.experimental.pallas import tpu as pltpu
from jax.sharding import PartitionSpec as P

GUARD_MAX = 4
TRAIN_MAX = 28
MARGIN = GUARD_MAX + TRAIN_MAX
EPSILON = 1e-06
INPUT_SCALE = 1.0 / 2048.0
LANES = 128
SUB = 8
RADIX = 4


def halves(table):
    hi = np.asarray(table, np.float32).astype(jnp.bfloat16)
    lo = (np.asarray(table, np.float64) - hi.astype(np.float64)).astype(jnp.bfloat16)
    return hi, lo


def lane_table(sign):
    idx = np.arange(LANES)
    ang = 2.0 * np.pi * ((idx[:, None] * idx[None, :]) % LANES) / LANES
    c, s = np.cos(ang), sign * np.sin(ang)
    full = np.block([[c, s], [-s, c]])
    hi, lo = halves(full)
    return np.concatenate([hi, hi, lo], axis=0)


def doppler_table(pulses):
    part = pulses // RADIX
    m = np.arange(part)
    out = []
    for res in range(RADIX):
        ang = 2.0 * np.pi * ((m[None, :] * (RADIX * m[:, None] + res)) % pulses) / pulses
        c, s = np.cos(ang) / math.sqrt(pulses), -np.sin(ang) / math.sqrt(pulses)
        full = np.block([[c, -s], [s, c]])
        hi, lo = halves(full)
        out.append(np.concatenate([hi, hi, lo], axis=1))
    return np.stack(out)


def split(x, axis):
    hi = x.astype(jnp.bfloat16)
    lo = (x - hi.astype(jnp.float32)).astype(jnp.bfloat16)
    return jnp.concatenate([hi, lo, hi], axis=axis)


def fft_list(re, im, sign):
    n = len(re)
    if n == 1:
        return re, im
    er, ei = fft_list(re[0::2], im[0::2], sign)
    odd_r, odd_i = fft_list(re[1::2], im[1::2], sign)
    half = n // 2
    out_r, out_i = [None] * n, [None] * n
    for k in range(half):
        a, b = odd_r[k], odd_i[k]
        if k == 0:
            tr, ti = a, b
        elif 4 * k == n:
            tr, ti = (b, -a) if sign < 0 else (-b, a)
        elif 8 * k == n or 8 * k == 3 * n:
            h = math.sqrt(0.5)
            c = h if 8 * k == n else -h
            tr = c * a - (sign * h) * b
            ti = c * b + (sign * h) * a
        else:
            c = math.cos(2.0 * math.pi * k / n)
            s = sign * math.sin(2.0 * math.pi * k / n)
            tr = c * a - s * b
            ti = s * a + c * b
        out_r[k], out_i[k] = er[k] + tr, ei[k] + ti
        out_r[k + half], out_i[k + half] = er[k] - tr, ei[k] - ti
    return out_r, out_i


def range_kernel(n, rows, x_ref, tw1, rep, tw2, wf, wi, *rest):
    outs = rest[:n]
    cols = x_ref.shape[-1] // LANES
    per = cols // n

    def body(g, carry):
        r0 = pl.multiple_of(g * SUB, SUB)
        re = [x_ref[0, 0, pl.ds(r0, SUB), a * LANES:(a + 1) * LANES].astype(jnp.float32) for a in range(cols)]
        im = [x_ref[1, 0, pl.ds(r0, SUB), a * LANES:(a + 1) * LANES].astype(jnp.float32) for a in range(cols)]
        re, im = fft_list(re, im, -1.0)
        mr, mi = jnp.concatenate(re, axis=0), jnp.concatenate(im, axis=0)
        tr, ti = tw1[0], tw1[1]
        m = jnp.concatenate([mr * tr - mi * ti, mr * ti + mi * tr], axis=1)
        f = jnp.dot(split(m, 1), wf[...], preferred_element_type=jnp.float32)
        fr, fi = f[:, :LANES], f[:, LANES:]
        tr, ti = rep[0], rep[1]
        m = jnp.concatenate([fr * tr - fi * ti, fr * ti + fi * tr], axis=1)
        f = jnp.dot(split(m, 1), wi[...], preferred_element_type=jnp.float32)
        fr, fi = f[:, :LANES], f[:, LANES:]
        tr, ti = tw2[0], tw2[1]
        mr, mi = fr * tr - fi * ti, fr * ti + fi * tr
        re = [mr[a * SUB:(a + 1) * SUB] for a in range(cols)]
        im = [mi[a * SUB:(a + 1) * SUB] for a in range(cols)]
        re, im = fft_list(re, im, 1.0)
        for j in range(n):
            for a in range(per):
                outs[j][0, pl.ds(r0, SUB), a * LANES:(a + 1) * LANES] = re[j * per + a]
                outs[j][1, pl.ds(r0, SUB), a * LANES:(a + 1) * LANES] = im[j * per + a]
        return carry

    lax.fori_loop(0, rows // SUB, body, 0, unroll=2)


def range_compress(n, channel, samples, tw1, rep, tw2, wf, wi):
    _, _, pulses, gates = samples.shape
    rows = min(32, pulses)
    whole = lambda a: pl.BlockSpec(a.shape, lambda i: (0,) * a.ndim)
    return pl.pallas_call(
        functools.partial(range_kernel, n, rows),
        grid=(pulses // rows,),
        in_specs=[pl.BlockSpec((2, 1, rows, gates), lambda i: (0, channel, i, 0))]
        + [whole(a) for a in (tw1, rep, tw2, wf, wi)],
        out_specs=[pl.BlockSpec((2, rows, gates // n), lambda i: (0, i, 0))] * n,
        out_shape=[jax.ShapeDtypeStruct((2, pulses, gates // n), jnp.float32)] * n,
        compiler_params=pltpu.CompilerParams(vmem_limit_bytes=40 << 20),
        cost_estimate=pl.CostEstimate(flops=int(3e9), bytes_accessed=16 << 20, transcendentals=0),
    )(samples, tw1, rep, tw2, wf, wi)


def doppler_kernel(x0, x1, x2, x3, t_ref, p_ref):
    part = x0.shape[1]
    a, b, c, d = ([x[0], x[1]] for x in (x0, x1, x2, x3))
    sr, si = a[0] + c[0], a[1] + c[1]
    dr, di = a[0] - c[0], a[1] - c[1]
    ur, ui = b[0] + d[0], b[1] + d[1]
    vr, vi = b[0] - d[0], b[1] - d[1]
    ys = [(sr + ur, si + ui), (dr + vi, di - vr), (sr - ur, si - ui), (dr - vi, di + vr)]
    for res in range(RADIX):
        y = jnp.concatenate(ys[res], axis=0)
        out = jnp.dot(t_ref[res], split(y, 0), preferred_element_type=jnp.float32)
        re, im = out[:part], out[part:]
        p_ref[res] = re * re + im * im


def doppler_power(blocks, table):
    _, part, gates = blocks[0].shape
    width = min(256, gates)
    return pl.pallas_call(
        doppler_kernel,
        grid=(gates // width,),
        in_specs=[pl.BlockSpec((2, part, width), lambda i: (0, 0, i))] * RADIX
        + [pl.BlockSpec(table.shape, lambda i: (0, 0, 0))],
        out_specs=pl.BlockSpec((RADIX, part, width), lambda i: (0, 0, i)),
        out_shape=jax.ShapeDtypeStruct((RADIX, part, gates), jnp.float32),
        compiler_params=pltpu.CompilerParams(vmem_limit_bytes=40 << 20),
        cost_estimate=pl.CostEstimate(flops=int(3e9), bytes_accessed=8 << 20, transcendentals=0),
    )(*blocks, table)


def cfar_kernel(channel, scale_ref, p_ref, l_ref, r_ref, band_ref, cells_ref, *rest):
    out_ref, sum_ref, turn = rest[-3:]
    _, rows, gates = p_ref.shape
    width = band_ref.shape[-1]
    total = RADIX * rows
    core = p_ref[...].reshape(total, gates)
    zeros = jnp.zeros((total, LANES - MARGIN), jnp.float32)
    padded = jnp.concatenate(
        [zeros, l_ref[...].reshape(total, MARGIN), core, r_ref[...].reshape(total, MARGIN), zeros], axis=1
    )
    hi = padded.astype(jnp.bfloat16)
    lo = (padded - hi.astype(jnp.float32)).astype(jnp.bfloat16)
    band = band_ref[0]
    inv = scale_ref[channel, 1].astype(jnp.float32) / scale_ref[channel, 0].astype(jnp.float32)
    acc = jnp.zeros((SUB, LANES), jnp.float32)
    for g in range(gates // width):
        cut = slice(g * width, (g + 1) * width + 2 * LANES)
        noise = jnp.dot(hi[:, cut], band, preferred_element_type=jnp.float32) + jnp.dot(
            lo[:, cut], band, preferred_element_type=jnp.float32
        )
        here = slice(g * width, (g + 1) * width)
        ratio = core[:, here] * cells_ref[0, :, here] / (noise + EPSILON)
        for c in range(width // LANES):
            lanes = slice(c * LANES, (c + 1) * LANES)
            for res in range(RADIX):
                turn[g, c, pl.ds(res, rows, stride=RADIX), :] = ratio[res * rows:(res + 1) * rows, lanes]
            out_ref[0, :, g * width + c * LANES:g * width + (c + 1) * LANES] = turn[g, c]
        soft = jnp.clip(ratio * inv - 1.0, 0.0, 1.0)
        for c in range(width // LANES):
            acc = acc + jnp.sum(soft[:, c * LANES:(c + 1) * LANES].reshape(total // SUB, SUB, LANES), axis=0)

    @pl.when(pl.program_id(0) == 0)
    def _():
        sum_ref[...] = jnp.zeros_like(sum_ref)

    sum_ref[...] += acc


def cfar(channel, channels, power, left, right, band, cells, thresh, prior):
    _, part, gates = power.shape
    rows = min(32, part)
    width = band.shape[-1]
    specs = [
        pl.BlockSpec(memory_space=pltpu.SMEM),
        pl.BlockSpec((RADIX, rows, gates), lambda i: (0, i, 0)),
        pl.BlockSpec((RADIX, rows, MARGIN), lambda i: (0, i, 0)),
        pl.BlockSpec((RADIX, rows, MARGIN), lambda i: (0, i, 0)),
        pl.BlockSpec((1,) + band.shape[1:], lambda i: (channel, 0, 0)),
        pl.BlockSpec((1,) + cells.shape[1:], lambda i: (channel, 0, 0)),
    ]
    args = [thresh, power, left, right, band, cells]
    aliases = {}
    if prior is not None:
        specs.append(pl.BlockSpec(memory_space=pl.ANY))
        args.append(prior)
        aliases = {6: 0}
    return pl.pallas_call(
        functools.partial(cfar_kernel, channel),
        grid=(part // rows,),
        in_specs=specs,
        out_specs=[
            pl.BlockSpec((1, RADIX * rows, gates), lambda i: (channel, i, 0)),
            pl.BlockSpec((SUB, LANES), lambda i: (0, 0)),
        ],
        out_shape=[
            jax.ShapeDtypeStruct((channels, RADIX * part, gates), jnp.float32),
            jax.ShapeDtypeStruct((SUB, LANES), jnp.float32),
        ],
        input_output_aliases=aliases,
        scratch_shapes=[pltpu.VMEM((gates // width, width // LANES, RADIX * rows, LANES), jnp.float32)],
        compiler_params=pltpu.CompilerParams(vmem_limit_bytes=40 << 20),
        cost_estimate=pl.CostEstimate(flops=int(2e9), bytes_accessed=5 << 20, transcendentals=0),
    )(*args)


def local(samples, replica, window, thresh):
    _, channels, part, gates = samples.shape
    n = lax.axis_size("pulse")
    me = lax.axis_index("pulse")
    cols = gates // LANES
    pulses = part * n
    own = gates // n

    k1 = np.arange(cols)[:, None]
    b = np.arange(LANES)[None, :]
    ang = 2.0 * np.pi * ((k1 * b) % gates) / gates
    tw1 = np.repeat(np.stack([np.cos(ang), -np.sin(ang)]), SUB, axis=1).astype(np.float32)
    turned = (jnp.asarray(k1 * b, jnp.int32) + own * me * jnp.asarray(k1, jnp.int32)) % gates
    ang2 = turned.astype(jnp.float32) * (2.0 * math.pi / gates)
    tw2 = jnp.repeat(jnp.stack([jnp.cos(ang2), jnp.sin(ang2)]), SUB, axis=1)
    rep = jnp.swapaxes(replica.reshape(2, LANES, cols), 1, 2) * (INPUT_SCALE / gates)
    rep = jnp.repeat(rep, SUB, axis=1)
    wf, wi = jnp.asarray(lane_table(-1.0)), jnp.asarray(lane_table(1.0))
    table = jnp.asarray(doppler_table(pulses))

    width = min(256, own)
    guard = window[:, 0][:, None, None]
    reach = guard + window[:, 1][:, None, None]
    dist = jnp.abs(
        jnp.arange(width + 2 * LANES, dtype=jnp.int32)[:, None] - LANES - jnp.arange(width, dtype=jnp.int32)[None, :]
    )[None]
    band = ((dist > guard) & (dist <= reach)).astype(jnp.bfloat16)
    gate = (me * own + jnp.arange(own, dtype=jnp.int32))[None, None, :]
    after = gates - 1 - gate
    cells = (
        jnp.minimum(gate, reach) - jnp.minimum(gate, guard) + jnp.minimum(after, reach) - jnp.minimum(after, guard)
    ).astype(jnp.float32)

    def shift(x, s):
        return lax.ppermute(x, "pulse", [(i, (i + s) % n) for i in range(n)])

    order = sorted(range(1, n), key=lambda s: -min(s, n - s))
    got = []
    for channel in range(channels):
        outs = range_compress(n, channel, samples, tw1, rep, tw2, wf, wi)
        blocks = [outs[0]] + [None] * (n - 1)
        for s in order:
            blocks[n - s] = shift(outs[s], s)
        got.append(blocks)

    ratio, sums = None, []
    up = [(i, i + 1) for i in range(n - 1)]
    down = [(i + 1, i) for i in range(n - 1)]
    for channel in range(channels):
        blocks = got[channel]
        if n != RADIX:
            full = jnp.concatenate(blocks, axis=1)
            blocks = [full[:, q * (pulses // RADIX):(q + 1) * (pulses // RADIX)] for q in range(RADIX)]
        power = doppler_power(blocks, table)
        left = lax.ppermute(power[:, :, own - MARGIN:], "pulse", up)
        right = lax.ppermute(power[:, :, :MARGIN], "pulse", down)
        ratio, part_sum = cfar(channel, channels, power, left, right, band, cells, thresh, ratio)
        sums.append(part_sum)
    total = jnp.sum(functools.reduce(jnp.add, sums)) * (1024.0 / (pulses * gates))
    everyone = lax.all_gather(total.reshape(1), ("pulse", "chan", "sub"), tiled=True)
    return (ratio, jnp.sum(everyone).reshape(1))


def solution(mesh):
    in_specs = (
        P(None, ("grp", "chan", "sub"), "pulse", None),
        P(),
        P(("grp", "chan", "sub"), None),
        P(("grp", "chan", "sub"), None),
    )
    out_specs = (P(("grp", "chan", "sub"), None, "pulse"), P("grp"))
    return jax.shard_map(local, mesh=mesh, in_specs=in_specs, out_specs=out_specs, check_vma=False)
```

time: 500 us -> 259 us (0.52); the launches traced: 493 us -> 258 us
  matrix products: 207 us -> 0 us
  starting transfers between devices: 14.2 us -> 106 us
  local copies, waits for them, and re-layouts: 96.2 us -> 15.2 us
  waiting for transfers between devices: 132 us -> 67.5 us
  Pallas kernels: 0 us -> 34.6 us
    dot_general x50 -> x0, matrix products: 207 us -> none  [the longest x12 50.4 us: complex_einsum(): jnp.einsum(form, x_re, t_re, precision=HIGHEST)]
    all_to_all x2 -> x0, waiting for transfers between devices: 131 us -> none  [local(): lax.all_to_all(stacked, 'pulse', split_axis=3, concat_axis=2, tiled=True)]
    ppermute x2 -> x10, starting transfers between devices: 2.97 us -> 106 us  [the longest x6 54.3 us: shift(): return lax.ppermute(x, 'pulse', [(i, (i + s) % n) for i in range(n)])]
    ppermute x2 -> x10, waiting for transfers between devices: 0.79 us -> 67.5 us  [the longest x6 63.1 us: shift(): return lax.ppermute(x, 'pulse', [(i, (i + s) % n) for i in range(n)])]
    another operation x2 -> x0, local copies, waits for them, and re-layouts: 38.3 us -> none  [local(): stacked = jnp.stack([comp_re, comp_im])]
    pallas_call x0 -> x6, Pallas kernels: none -> 34.6 us  [the longest x2 17.8 us: range_compress(): pl.pallas_call(functools.partial(range_kernel, n, rows), grid=(pulses //...]
    psum x1 -> x0, blocking collectives: 32.9 us -> none  [local(): detections = lax.psum(partial_sum, ('pulse', 'chan', 'sub'))]
    unnamed x0 -> x1, blocking collectives: none -> 29.5 us
  transfers between devices with their start and end apart: 4 -> 10, of which waited for: 3 -> 4; matrix products, arithmetic and copies ran while one was open for 12% -> 1% of each run, Pallas kernels for 0% -> 8%
where the time goes in v1:
time: 259 us; the launch traced here: 258 us
  starting transfers between devices  106 us (41%)
  waiting for transfers between devices  67.5 us (26%)
  Pallas kernels  34.6 us (13%)
  blocking collectives  29.5 us (11%)
  local copies, waits for them, and re-layouts  15.2 us (6%)
  other arithmetic  3.99 us (2%)
    ppermute x6, waiting for transfers between devices, shift(): return lax.ppermute(x, 'pulse', [(i, (i + s) % n) for i in range(n)])  63.1 us
    ppermute x6, starting transfers between devices, shift(): return lax.ppermute(x, 'pulse', [(i, (i + s) % n) for i in range(n)])  54.3 us
    ppermute x2, starting transfers between devices, local(): left = lax.ppermute(power[:, :, own - MARGIN:], 'pulse', up)  48.8 us
    unnamed x1, blocking collectives  29.5 us
    pallas_call x2, Pallas kernels, range_compress(): pl.pallas_call(functools.partial(range_kernel, n, rows), grid=(pulses //...  17.8 us
    unnamed x33, local copies, waits for them, and re-layouts  14.5 us
    pallas_call x2, Pallas kernels, doppler_power(): pl.pallas_call(doppler_kernel, grid=(gates // width,), in_specs=[pl.Block...  9.1 us
    pallas_call x2, Pallas kernels, cfar(): pl.pallas_call(functools.partial(cfar_kernel, channel), grid=(part // row...  7.62 us
  transfers between devices with their start and end apart: 10, of which 4 were waited for; matrix products, arithmetic and copies ran while one was open for 1% of the time, Pallas kernels for 8%

profile of v1, /device:TPU:0, one launch (start us, length us, event | category | flops | bytes accessed | tf_op | source)
XLA Modules:
  0.0 257.9 jit_solution(8084630942541299560)
XLA Ops:
  0.6 0.8 broadcast_multiply_fusion
  2.3 0.9 cosine_bitcast_fusion
  3.2 3.4 %copy-done = s32[2,2,128,4096]{3,2,1,0:T(8,128)S(1)} copy-done((s32[2,2,128,4096]{3,2,1,0:T(8,128)S(1)}, s32[2,2,128,4096]{3,2,1,0:T(8,128)}, u32[]{:S(2)}) %copy-start) | copy-done | bytes 8388632
  6.6 1.0 copy-done.6
  7.6 1.0 copy-done.7
  8.6 0.9 copy-done.8
  9.5 8.9 %shard_map.115 = (f32[2,128,1024]{2,1,0:T(8,128)S(1)}, f32[2,128,1024]{2,1,0:T(8,128)}, f32[2,128,1024]{2,1,0:T(8,128)}, f32[2,128,1024]{2,1,0:T(8,128)S(1)}) custom-call(s32[2,2,128,4096]{3,2,1,0:T(8,128)S(1)} %copy-done, f32[2,256,128]{2,1,0:T(8,128)S(1)} %copy-done.8, f32[2,256,128]{2,1,0:T(8,128)S(1)} %get-tuple-element.37.rep, ...), custom_call_target="tpu_custom_call" | custom-call | flops 3000000000 | bytes 16777216 | tf_op jit(solution)/shard_map/pallas_call | solution.py:122
  18.5 1.0 copy-done.11
  19.4 5.1 %collective-permute-start.5 = (f32[2,128,1024]{2,1,0:T(8,128)S(1)}, f32[2,128,1024]{2,1,0:T(8,128)S(1)}, u32[]{:S(2)}, u32[]{:S(2)}) collective-permute-start(f32[2,128,1024]{2,1,0:T(8,128)S(1)} %get-tuple-element.19), channel_id=1, source_target_pairs={{0,12},{4,0},{8,4},{12,8},{1,13},{5,1},{9,5},{13,9},{2,14},{6,2},{... | collective-permute-start | bytes 3145736 | tf_op jit(solution)/shard_map/ppermute | solution.py:273
  24.5 1.0 collective-permute-start.7
  25.5 8.9 %shard_map.113 = (f32[2,128,1024]{2,1,0:T(8,128)S(1)}, f32[2,128,1024]{2,1,0:T(8,128)S(1)}, f32[2,128,1024]{2,1,0:T(8,128)S(1)}, f32[2,128,1024]{2,1,0:T(8,128)}) custom-call(s32[2,2,128,4096]{3,2,1,0:T(8,128)S(1)} %copy-done, f32[2,256,128]{2,1,0:T(8,128)S(1)} %copy-done.8, f32[2,256,128]{2,1,0:T(8,128)S(1)} %get-tuple-element.37.rep, ...), custom_call_target="tpu_custom_call" | custom-call | flops 3000000000 | bytes 16777216 | tf_op jit(solution)/shard_map/pallas_call | solution.py:122
  34.5 1.0 copy-done.9
  35.4 2.8 %collective-permute-start = (f32[2,128,1024]{2,1,0:T(8,128)}, f32[2,128,1024]{2,1,0:T(8,128)S(1)}, u32[]{:S(2)}, u32[]{:S(2)}) collective-permute-start(f32[2,128,1024]{2,1,0:T(8,128)} %get-tuple-element.15), channel_id=1, source_target_pairs={{0,12},{4,0},{8,4},{12,8},{1,13},{5,1},{9,5},{13,9},{2,14},{6,2},{... | collective-permute-start | bytes 3145736 | tf_op jit(solution)/shard_map/ppermute | solution.py:273
  38.3 1.1 collective-permute-start.1
  39.7 8.4 %collective-permute-done.5.x1 = f32[2,128,1024]{2,1,0:T(8,128)S(1)} collective-permute-done((f32[2,128,1024]{2,1,0:T(8,128)S(1)}, f32[2,128,1024]{2,1,0:T(8,128)S(1)}, u32[]{:S(2)}, u32[]{:S(2)}) %collective-permute-start.5) | collective-permute-done | bytes 1048608 | tf_op jit(solution)/shard_map/ppermute | solution.py:273
  48.1 1.1 copy-done.1
  49.2 44.3 %collective-permute-start.2 = (f32[2,128,1024]{2,1,0:T(8,128)S(1)}, f32[2,128,1024]{2,1,0:T(8,128)}, u32[]{:S(2)}, u32[]{:S(2)}) collective-permute-start(f32[2,128,1024]{2,1,0:T(8,128)S(1)} %get-tuple-element.17), channel_id=1, source_target_pairs={{0,4},{4,8},{8,12},{12,0},{1,5},{5,9},{9,13},{13,1},{2,6},{6,10},{... | collective-permute-start | bytes 3145736 | tf_op jit(solution)/shard_map/ppermute | solution.py:273
  94.4 22.2 %collective-permute-done.6.x2 = f32[2,128,1024]{2,1,0:T(8,128)} collective-permute-done((f32[2,128,1024]{2,1,0:T(8,128)}, f32[2,128,1024]{2,1,0:T(8,128)}, u32[]{:S(2)}, u32[]{:S(2)}) %collective-permute-start.6) | collective-permute-done | bytes 1048608 | tf_op jit(solution)/shard_map/ppermute | solution.py:273
  116.6 1.2 copy-done.2
  117.9 1.4 copy-done.4
  119.3 1.2 copy-done.12
  120.5 4.6 %shard_map.116.p_ref = f32[4,128,1024]{2,1,0:T(8,128)S(1)} custom-call(f32[2,128,1024]{2,1,0:T(8,128)S(1)} %copy-done.12, f32[2,128,1024]{2,1,0:T(8,128)S(1)} %copy-done.2, f32[2,128,1024]{2,1,0:T(8,128)} %collective-permute-done.6.x2, f32[2,128,1024]{2,1,0:T(8,128)} %collective-permute-done.7.x3, bf16[4,256,768]{2,1,0:T(8,128)(2,1)S(1)} %copy-done.4), custom_call_target="tpu_custom_call" | custom-call | flops 3000000000 | bytes 8388608 | tf_op jit(solution)/shard_map/pallas_call | solution.py:152
  125.3 46.3 %collective-permute-start.8 = (f32[4,128,32]{2,1,0:T(8,128)S(1)}, f32[4,128,32]{2,1,0:T(8,128)S(1)}, u32[]{:S(2)}, u32[]{:S(2)}) collective-permute-start(f32[4,128,32]{2,1,0:T(8,128)S(1)} %get-tuple-element.29), channel_id=1, source_target_pairs={{0,4},{4,8},{8,12},{1,5},{5,9},{9,13},{2,6},{6,10},{10,14},{3,7},{... | collective-permute-start | bytes 196616 | tf_op jit(solution)/shard_map/ppermute | solution.py:293
  171.6 1.3 collective-permute-start.9
  172.9 32.4 %collective-permute-done.1.x2 = f32[2,128,1024]{2,1,0:T(8,128)} collective-permute-done((f32[2,128,1024]{2,1,0:T(8,128)S(1)}, f32[2,128,1024]{2,1,0:T(8,128)}, u32[]{:S(2)}, u32[]{:S(2)}) %collective-permute-start.1) | collective-permute-done | bytes 1048608 | tf_op jit(solution)/shard_map/ppermute | solution.py:273
  205.4 4.5 %shard_map.114.p_ref = f32[4,128,1024]{2,1,0:T(8,128)S(1)} custom-call(f32[2,128,1024]{2,1,0:T(8,128)S(1)} %copy-done.10, f32[2,128,1024]{2,1,0:T(8,128)S(1)} %collective-permute-done.x1, f32[2,128,1024]{2,1,0:T(8,128)} %collective-permute-done.1.x2, f32[2,128,1024]{2,1,0:T(8,128)} %collective-permute-done.2.x3, bf16[4,256,768]{2,1,0:T(8,128)(2,1)S(1)} %copy-done.5), custom_call_target="tpu_custom_call" | custom-call | flops 3000000000 | bytes 8388608 | tf_op jit(solution)/shard_map/pallas_call | solution.py:152
  210.0 2.5 collective-permute-start.3
  212.5 1.3 collective-permute-start.4
  213.8 3.8 %shard_map.117 = (f32[2,512,1024]{2,1,0:T(8,128)}, f32[8,128]{1,0:T(8,128)S(1)}) custom-call(s32[2,2]{1,0:T(2,128)S(1)} %copy-done.3, f32[4,128,1024]{2,1,0:T(8,128)S(1)} %shard_map.116.p_ref, f32[4,128,32]{2,1,0:T(8,128)S(1)} %collective-permute-done.8.l_ref, f32[4,128,32]{2,1,0:T(8,128)S(1)} %collective-permute-done.9.r_ref, ...), custom_call_target="tpu_custom_call" | custom-call | flops 2000000000 | bytes 5242880 | tf_op jit(solution)/shard_map/pallas_call | solution.py:220
  217.6 4.4 %collective-permute-done.4.r_ref = f32[4,128,32]{2,1,0:T(8,128)S(1)} collective-permute-done((f32[4,128,32]{2,1,0:T(8,128)S(1)}, f32[4,128,32]{2,1,0:T(8,128)S(1)}, u32[]{:S(2)}, u32[]{:S(2)}) %collective-permute-start.4) | collective-permute-done | bytes 65568 | tf_op jit(solution)/shard_map/ppermute | solution.py:294
  222.0 3.8 %shard_map.118 = (f32[2,512,1024]{2,1,0:T(8,128)}, f32[8,128]{1,0:T(8,128)S(1)}) custom-call(s32[2,2]{1,0:T(2,128)S(1)} %copy-done.3, f32[4,128,1024]{2,1,0:T(8,128)S(1)} %shard_map.114.p_ref, f32[4,128,32]{2,1,0:T(8,128)S(1)} %collective-permute-done.3.l_ref, f32[4,128,32]{2,1,0:T(8,128)S(1)} %collective-permute-done.4.r_ref, ...), custom_call_target="tpu_custom_call", output_to_operand_aliasing={{0}: (6, {})} | custom-call | flops 2000000000 | bytes 5242880 | tf_op jit(solution)/shard_map/pallas_call | solution.py:220
  227.8 29.5 %all-reduce = f32[16]{0:T(128)S(1)} all-reduce(f32[16]{0:T(128)S(1)} %dynamic-update-slice), channel_id=1, replica_groups=mesh['grp'=2,'pulse'=4,'chan'=2,'sub'=2] {'pulse','chan','sub'}, use_global_device_ids=true, to_apply=%add | all-reduce | flops 16 | bytes 128
  (46 shorter events, 4.4 us)
Async XLA Ops:
  3.2 3.4 %copy-start = (s32[2,2,128,4096]{3,2,1,0:T(8,128)S(1)}, s32[2,2,128,4096]{3,2,1,0:T(8,128)}, u32[]{:S(2)}) copy-start(s32[2,2,128,4096]{3,2,1,0:T(8,128)} %x_ref.3) | copy-start | bytes 25165828
  6.6 1.0 copy-start.6
  7.6 1.0 copy-start.7
  8.6 0.9 copy-start.8
  18.5 1.0 copy-start.11
  19.4 28.7 %collective-permute-start.5 = (f32[2,128,1024]{2,1,0:T(8,128)S(1)}, f32[2,128,1024]{2,1,0:T(8,128)S(1)}, u32[]{:S(2)}, u32[]{:S(2)}) collective-permute-start(f32[2,128,1024]{2,1,0:T(8,128)S(1)} %get-tuple-element.19), channel_id=1, source_target_pairs={{0,12},{4,0},{8,4},{12,8},{1,13},{5,1},{9,5},{13,9},{2,14},{6,2},{... | collective-permute-start | bytes 3145736 | tf_op jit(solution)/shard_map/ppermute | solution.py:273
  24.5 92.1 %collective-permute-start.6 = (f32[2,128,1024]{2,1,0:T(8,128)}, f32[2,128,1024]{2,1,0:T(8,128)}, u32[]{:S(2)}, u32[]{:S(2)}) collective-permute-start(f32[2,128,1024]{2,1,0:T(8,128)} %get-tuple-element.20), channel_id=1, source_target_pairs={{0,8},{4,12},{8,0},{12,4},{1,9},{5,13},{9,1},{13,5},{2,10},{6,14},... | collective-permute-start | bytes 3145736 | tf_op jit(solution)/shard_map/ppermute | solution.py:273
  24.5 14.9 %copy-start.13 = (s32[2,2]{1,0:T(2,128)S(1)}, s32[2,2]{1,0:T(2,128)}, u32[]{:S(2)}) copy-start(s32[2,2]{1,0:T(2,128)} %param.12) | copy-start | bytes 52
  24.5 69.0 %copy-start.14 = (u32[32]{0:T(128)S(1)}, u32[32]{0:T(128)}, u32[]{:S(2)}) copy-start(u32[32]{0:T(128)} %constant.57) | copy-start | bytes 388
  24.5 92.1 %collective-permute-start.7 = (f32[2,128,1024]{2,1,0:T(8,128)}, f32[2,128,1024]{2,1,0:T(8,128)}, u32[]{:S(2)}, u32[]{:S(2)}) collective-permute-start(f32[2,128,1024]{2,1,0:T(8,128)} %get-tuple-element.21), channel_id=1, source_target_pairs={{0,4},{4,8},{8,12},{12,0},{1,5},{5,9},{9,13},{13,1},{2,6},{6,10},{... | collective-permute-start | bytes 3145736 | tf_op jit(solution)/shard_map/ppermute | solution.py:273
  34.5 1.0 copy-start.9
  35.4 137.5 %collective-permute-start = (f32[2,128,1024]{2,1,0:T(8,128)}, f32[2,128,1024]{2,1,0:T(8,128)S(1)}, u32[]{:S(2)}, u32[]{:S(2)}) collective-permute-start(f32[2,128,1024]{2,1,0:T(8,128)} %get-tuple-element.15), channel_id=1, source_target_pairs={{0,12},{4,0},{8,4},{12,8},{1,13},{5,1},{9,5},{13,9},{2,14},{6,2},{... | collective-permute-start | bytes 3145736 | tf_op jit(solution)/shard_map/ppermute | solution.py:273
  38.3 167.1 %collective-permute-start.1 = (f32[2,128,1024]{2,1,0:T(8,128)S(1)}, f32[2,128,1024]{2,1,0:T(8,128)}, u32[]{:S(2)}, u32[]{:S(2)}) collective-permute-start(f32[2,128,1024]{2,1,0:T(8,128)S(1)} %get-tuple-element.16), channel_id=1, source_target_pairs={{0,8},{4,12},{8,0},{12,4},{1,9},{5,13},{9,1},{13,5},{2,10},{6,14},... | collective-permute-start | bytes 3145736 | tf_op jit(solution)/shard_map/ppermute | solution.py:273
  48.1 1.1 copy-start.1
  49.2 156.2 %collective-permute-start.2 = (f32[2,128,1024]{2,1,0:T(8,128)S(1)}, f32[2,128,1024]{2,1,0:T(8,128)}, u32[]{:S(2)}, u32[]{:S(2)}) collective-permute-start(f32[2,128,1024]{2,1,0:T(8,128)S(1)} %get-tuple-element.17), channel_id=1, source_target_pairs={{0,4},{4,8},{8,12},{12,0},{1,5},{5,9},{9,13},{13,1},{2,6},{6,10},{... | collective-permute-start | bytes 3145736 | tf_op jit(solution)/shard_map/ppermute | solution.py:273
  116.6 1.2 copy-start.2
  117.9 1.4 copy-start.4
  119.3 1.2 copy-start.12
  120.5 84.9 %copy-start.5 = (bf16[4,256,768]{2,1,0:T(8,128)(2,1)S(1)}, bf16[4,256,768]{2,1,0:T(8,128)(2,1)}, u32[]{:S(2)}) copy-start(bf16[4,256,768]{2,1,0:T(8,128)(2,1)} %constant.50.clone.t_ref) | copy-start | bytes 4718596
  120.5 84.9 %copy-start.10 = (f32[2,128,1024]{2,1,0:T(8,128)S(1)}, f32[2,128,1024]{2,1,0:T(8,128)}, u32[]{:S(2)}) copy-start(f32[2,128,1024]{2,1,0:T(8,128)} %copy-done.9) | copy-start | bytes 3145732
  125.3 88.5 %collective-permute-start.8 = (f32[4,128,32]{2,1,0:T(8,128)S(1)}, f32[4,128,32]{2,1,0:T(8,128)S(1)}, u32[]{:S(2)}, u32[]{:S(2)}) collective-permute-start(f32[4,128,32]{2,1,0:T(8,128)S(1)} %get-tuple-element.29), channel_id=1, source_target_pairs={{0,4},{4,8},{8,12},{1,5},{5,9},{9,13},{2,6},{6,10},{10,14},{3,7},{... | collective-permute-start | bytes 196616 | tf_op jit(solution)/shard_map/ppermute | solution.py:293
  171.6 42.2 %collective-permute-start.9 = (f32[4,128,32]{2,1,0:T(8,128)S(1)}, f32[4,128,32]{2,1,0:T(8,128)S(1)}, u32[]{:S(2)}, u32[]{:S(2)}) collective-permute-start(f32[4,128,32]{2,1,0:T(8,128)S(1)} %get-tuple-element.28), channel_id=1, source_target_pairs={{4,0},{8,4},{12,8},{5,1},{9,5},{13,9},{6,2},{10,6},{14,10},{7,3},{... | collective-permute-start | bytes 196616 | tf_op jit(solution)/shard_map/ppermute | solution.py:294
  205.4 8.4 %copy-start.3 = (s32[2,2]{1,0:T(2,128)S(1)}, s32[2,2]{1,0:T(2,128)}, u32[]{:S(2)}) copy-start(s32[2,2]{1,0:T(2,128)} %scale_ref.3) | copy-start | bytes 52
  210.0 7.6 %collective-permute-start.3 = (f32[4,128,32]{2,1,0:T(8,128)S(1)}, f32[4,128,32]{2,1,0:T(8,128)S(1)}, u32[]{:S(2)}, u32[]{:S(2)}) collective-permute-start(f32[4,128,32]{2,1,0:T(8,128)S(1)} %get-tuple-element.31), channel_id=1, source_target_pairs={{0,4},{4,8},{8,12},{1,5},{5,9},{9,13},{2,6},{6,10},{10,14},{3,7},{... | collective-permute-start | bytes 196616 | tf_op jit(solution)/shard_map/ppermute | solution.py:293
  212.5 9.6 %collective-permute-start.4 = (f32[4,128,32]{2,1,0:T(8,128)S(1)}, f32[4,128,32]{2,1,0:T(8,128)S(1)}, u32[]{:S(2)}, u32[]{:S(2)}) collective-permute-start(f32[4,128,32]{2,1,0:T(8,128)S(1)} %get-tuple-element.30), channel_id=1, source_target_pairs={{4,0},{8,4},{12,8},{5,1},{9,5},{13,9},{6,2},{10,6},{14,10},{7,3},{... | collective-permute-start | bytes 196616 | tf_op jit(solution)/shard_map/ppermute | solution.py:294

commit v2 on v1

--- a/solution.py
+++ b/solution.py
@@ -126,7 +126,7 @@
         + [whole(a) for a in (tw1, rep, tw2, wf, wi)],
         out_specs=[pl.BlockSpec((2, rows, gates // n), lambda i: (0, i, 0))] * n,
         out_shape=[jax.ShapeDtypeStruct((2, pulses, gates // n), jnp.float32)] * n,
-        compiler_params=pltpu.CompilerParams(vmem_limit_bytes=40 << 20),
+        compiler_params=pltpu.CompilerParams(vmem_limit_bytes=60 << 20),
         cost_estimate=pl.CostEstimate(flops=int(3e9), bytes_accessed=16 << 20, transcendentals=0),
     )(samples, tw1, rep, tw2, wf, wi)
 
@@ -236,6 +236,17 @@
     )(*args)
 
 
+def sum_over(x, axis):
+    size = lax.axis_size(axis)
+    if size & (size - 1):
+        return lax.psum(x, axis)
+    bit = 1
+    while bit < size:
+        x = x + lax.ppermute(x, axis, [(i, i ^ bit) for i in range(size)])
+        bit *= 2
+    return x
+
+
 def local(samples, replica, window, thresh):
     _, channels, part, gates = samples.shape
     n = lax.axis_size("pulse")
@@ -286,6 +297,8 @@
     down = [(i + 1, i) for i in range(n - 1)]
     for channel in range(channels):
         blocks = got[channel]
+        if sums:
+            blocks, sums = lax.optimization_barrier((blocks, sums))
         if n != RADIX:
             full = jnp.concatenate(blocks, axis=1)
             blocks = [full[:, q * (pulses // RADIX):(q + 1) * (pulses // RADIX)] for q in range(RADIX)]
@@ -295,8 +308,10 @@
         ratio, part_sum = cfar(channel, channels, power, left, right, band, cells, thresh, ratio)
         sums.append(part_sum)
     total = jnp.sum(functools.reduce(jnp.add, sums)) * (1024.0 / (pulses * gates))
-    everyone = lax.all_gather(total.reshape(1), ("pulse", "chan", "sub"), tiled=True)
-    return (ratio, jnp.sum(everyone).reshape(1))
+    count = total.reshape(1)
+    for axis in ("sub", "chan", "pulse"):
+        count = sum_over(count, axis)
+    return (ratio, count)
 
 
 def solution(mesh):

time: 259 us -> 246 us (0.950)
  blocking collectives: 29.5 us -> 0 us
  starting transfers between devices: 106 us -> 129 us
  local copies, waits for them, and re-layouts: 15.2 us -> 4.13 us
  between operations: 1.49 us -> 5.08 us
    unnamed x1 -> x0, blocking collectives: 29.5 us -> none
    ppermute x0 -> x4, starting transfers between devices: none -> 13 us  [sum_over(): x = x + lax.ppermute(x, axis, [(i, i ^ bit) for i in range(size)])]
    unnamed x33 -> x12, local copies, waits for them, and re-layouts: 14.5 us -> 2.65 us
    ppermute x2, starting transfers between devices: 48.8 us -> 58.9 us  [local(): left = lax.ppermute(power[:, :, own - MARGIN:], 'pulse', up)]
    ppermute x6, waiting for transfers between devices: 63.1 us -> 58.3 us  [shift(): return lax.ppermute(x, 'pulse', [(i, (i + s) % n) for i in range(n)])]
    pallas_call x2, Pallas kernels: 17.8 us -> 20.8 us  [range_compress(): pl.pallas_call(functools.partial(range_kernel, n, rows), grid=(pulses //...]
  transfers between devices with their start and end apart: 10 -> 14, of which waited for: 4 -> 11; matrix products, arithmetic and copies ran while one was open for 1% -> 0% of each run, Pallas kernels for 8% -> 7%
where the time goes in v2:
time: 246 us
  starting transfers between devices  129 us (52%)
  waiting for transfers between devices  69.3 us (28%)
  Pallas kernels  35.1 us (14%)
  between operations  5.08 us (2%)
  local copies, waits for them, and re-layouts  4.13 us (2%)
  other arithmetic  3.39 us (1%)
    ppermute x2, starting transfers between devices, local(): left = lax.ppermute(power[:, :, own - MARGIN:], 'pulse', up)  58.9 us
    ppermute x6, waiting for transfers between devices, shift(): return lax.ppermute(x, 'pulse', [(i, (i + s) % n) for i in range(n)])  58.3 us
    ppermute x6, starting transfers between devices, shift(): return lax.ppermute(x, 'pulse', [(i, (i + s) % n) for i in range(n)])  54.2 us
    pallas_call x2, Pallas kernels, range_compress(): pl.pallas_call(functools.partial(range_kernel, n, rows), grid=(pulses //...  20.8 us
    ppermute x4, starting transfers between devices, sum_over(): x = x + lax.ppermute(x, axis, [(i, i ^ bit) for i in range(size)])  13 us
    pallas_call x2, Pallas kernels, cfar(): pl.pallas_call(functools.partial(cfar_kernel, channel), grid=(part // row...  7.61 us
    ppermute x2, waiting for transfers between devices, local(): right = lax.ppermute(power[:, :, :MARGIN], 'pulse', down)  6.67 us
    pallas_call x2, Pallas kernels, doppler_power(): pl.pallas_call(doppler_kernel, grid=(gates // width,), in_specs=[pl.Block...  6.62 us
  transfers between devices with their start and end apart: 14, of which 11 were waited for; matrix products, arithmetic and copies ran while one was open for 0% of the time, Pallas kernels for 7%

profile of v2, /device:TPU:0, one launch (start us, length us, event | category | flops | bytes accessed | tf_op | source)
XLA Modules:
  0.0 245.7 jit_solution(13699785625243053718)
XLA Ops:
  0.6 0.8 broadcast_multiply_fusion
  2.3 0.9 cosine_bitcast_fusion
  3.1 0.8 broadcast_bitcast_fusion
  4.0 10.4 %shard_map.114 = (f32[2,128,1024]{2,1,0:T(8,128)}, f32[2,128,1024]{2,1,0:T(8,128)}, f32[2,128,1024]{2,1,0:T(8,128)}, f32[2,128,1024]{2,1,0:T(8,128)}) custom-call(s32[2,2,128,4096]{3,2,1,0:T(8,128)} %x_ref.3, f32[2,256,128]{2,1,0:T(8,128)} %constant.51.clone.tw1, f32[2,256,128]{2,1,0:T(8,128)} %get-tuple-element.47.rep, ...), custom_call_target="tpu_custom_call" | custom-call | flops 3000000000 | bytes 16777216 | tf_op jit(solution)/shard_map/pallas_call | solution.py:122
  14.4 5.1 %collective-permute-start.3 = (f32[2,128,1024]{2,1,0:T(8,128)}, f32[2,128,1024]{2,1,0:T(8,128)S(1)}, u32[]{:S(2)}, u32[]{:S(2)}) collective-permute-start(f32[2,128,1024]{2,1,0:T(8,128)} %get-tuple-element.24), channel_id=1, source_target_pairs={{0,12},{4,0},{8,4},{12,8},{1,13},{5,1},{9,5},{13,9},{2,14},{6,2},{... | collective-permute-start | bytes 3145736 | tf_op jit(solution)/shard_map/ppermute | solution.py:284
  19.5 1.0 collective-permute-start.5
  20.5 10.4 %shard_map.113 = (f32[2,128,1024]{2,1,0:T(8,128)}, f32[2,128,1024]{2,1,0:T(8,128)}, f32[2,128,1024]{2,1,0:T(8,128)}, f32[2,128,1024]{2,1,0:T(8,128)}) custom-call(s32[2,2,128,4096]{3,2,1,0:T(8,128)} %x_ref.3, f32[2,256,128]{2,1,0:T(8,128)} %constant.51.clone.tw1, f32[2,256,128]{2,1,0:T(8,128)} %get-tuple-element.47.rep, ...), custom_call_target="tpu_custom_call" | custom-call | flops 3000000000 | bytes 16777216 | tf_op jit(solution)/shard_map/pallas_call | solution.py:122
  30.9 2.8 %collective-permute-start = (f32[2,128,1024]{2,1,0:T(8,128)}, f32[2,128,1024]{2,1,0:T(8,128)S(1)}, u32[]{:S(2)}, u32[]{:S(2)}) collective-permute-start(f32[2,128,1024]{2,1,0:T(8,128)} %get-tuple-element.20), channel_id=1, source_target_pairs={{0,12},{4,0},{8,4},{12,8},{1,13},{5,1},{9,5},{13,9},{2,14},{6,2},{... | collective-permute-start | bytes 3145736 | tf_op jit(solution)/shard_map/ppermute | solution.py:284
  33.7 1.1 collective-permute-start.1
  35.4 7.9 %collective-permute-done.3.x1 = f32[2,128,1024]{2,1,0:T(8,128)S(1)} collective-permute-done((f32[2,128,1024]{2,1,0:T(8,128)}, f32[2,128,1024]{2,1,0:T(8,128)S(1)}, u32[]{:S(2)}, u32[]{:S(2)}) %collective-permute-start.3) | collective-permute-done | bytes 1048608 | tf_op jit(solution)/shard_map/ppermute | solution.py:284
  43.4 44.2 %collective-permute-start.2 = (f32[2,128,1024]{2,1,0:T(8,128)}, f32[2,128,1024]{2,1,0:T(8,128)S(1)}, u32[]{:S(2)}, u32[]{:S(2)}) collective-permute-start(f32[2,128,1024]{2,1,0:T(8,128)} %get-tuple-element.22), channel_id=1, source_target_pairs={{0,4},{4,8},{8,12},{12,0},{1,5},{5,9},{9,13},{13,1},{2,6},{6,10},{... | collective-permute-start | bytes 3145736 | tf_op jit(solution)/shard_map/ppermute | solution.py:284
  87.6 24.1 %collective-permute-done.4.x2 = f32[2,128,1024]{2,1,0:T(8,128)S(1)} collective-permute-done((f32[2,128,1024]{2,1,0:T(8,128)}, f32[2,128,1024]{2,1,0:T(8,128)S(1)}, u32[]{:S(2)}, u32[]{:S(2)}) %collective-permute-start.4) | collective-permute-done | bytes 1048608 | tf_op jit(solution)/shard_map/ppermute | solution.py:284
  111.7 1.4 copy-done.1
  113.1 1.2 copy-done.4
  114.3 3.3 %shard_map.115.p_ref = f32[4,128,1024]{2,1,0:T(8,128)S(1)} custom-call(f32[2,128,1024]{2,1,0:T(8,128)S(1)} %copy-done.4, f32[2,128,1024]{2,1,0:T(8,128)S(1)} %collective-permute-done.3.x1, f32[2,128,1024]{2,1,0:T(8,128)S(1)} %collective-permute-done.4.x2, f32[2,128,1024]{2,1,0:T(8,128)S(1)} %collective-permute-done.5.x3, bf16[4,256,768]{2,1,0:T(8,128)(2,1)S(1)} %copy-done.1), custom_call_target="tpu_custom_call" | custom-call | flops 3000000000 | bytes 8388608 | tf_op jit(solution)/shard_map/pallas_call | solution.py:152
  117.8 1.3 collective-permute-start.7
  119.1 47.1 %collective-permute-start.6 = (f32[4,128,32]{2,1,0:T(8,128)S(1)}, f32[4,128,32]{2,1,0:T(8,128)S(1)}, u32[]{:S(2)}, u32[]{:S(2)}) collective-permute-start(f32[4,128,32]{2,1,0:T(8,128)S(1)} %get-tuple-element.41), channel_id=1, source_target_pairs={{0,4},{4,8},{8,12},{1,5},{5,9},{9,13},{2,6},{6,10},{10,14},{3,7},{... | collective-permute-start | bytes 196616 | tf_op jit(solution)/shard_map/ppermute | solution.py:306
  166.3 2.9 %collective-permute-done.7.r_ref = f32[4,128,32]{2,1,0:T(8,128)S(1)} collective-permute-done((f32[4,128,32]{2,1,0:T(8,128)S(1)}, f32[4,128,32]{2,1,0:T(8,128)S(1)}, u32[]{:S(2)}, u32[]{:S(2)}) %collective-permute-start.7) | collective-permute-done | bytes 65568 | tf_op jit(solution)/shard_map/ppermute | solution.py:307
  169.1 1.2 collective-permute-done.6.l_ref
  170.3 3.8 %shard_map.116 = (f32[2,512,1024]{2,1,0:T(8,128)}, f32[8,128]{1,0:T(8,128)S(1)}) custom-call(s32[2,2]{1,0:T(2,128)S(1)} %copy-done, f32[4,128,1024]{2,1,0:T(8,128)S(1)} %shard_map.115.p_ref, f32[4,128,32]{2,1,0:T(8,128)S(1)} %collective-permute-done.6.l_ref, f32[4,128,32]{2,1,0:T(8,128)S(1)} %collective-permute-done.7.r_ref, ...), custom_call_target="tpu_custom_call" | custom-call | flops 2000000000 | bytes 5242880 | tf_op jit(solution)/shard_map/pallas_call | solution.py:220
  174.1 26.3 %collective-permute-done.1.x2 = f32[2,128,1024]{2,1,0:T(8,128)S(1)} collective-permute-done((f32[2,128,1024]{2,1,0:T(8,128)}, f32[2,128,1024]{2,1,0:T(8,128)S(1)}, u32[]{:S(2)}, u32[]{:S(2)}) %collective-permute-start.1) | collective-permute-done | bytes 1048608 | tf_op jit(solution)/shard_map/ppermute | solution.py:284
  200.4 3.3 %shard_map.117.p_ref = f32[4,128,1024]{2,1,0:T(8,128)S(1)} custom-call(f32[2,128,1024]{2,1,0:T(8,128)S(1)} %copy-done.3, f32[2,128,1024]{2,1,0:T(8,128)S(1)} %collective-permute-done.x1, f32[2,128,1024]{2,1,0:T(8,128)S(1)} %collective-permute-done.1.x2, f32[2,128,1024]{2,1,0:T(8,128)S(1)} %collective-permute-done.2.x3, bf16[4,256,768]{2,1,0:T(8,128)(2,1)S(1)} %copy-done.2), custom_call_target="tpu_custom_call" | custom-call | flops 3000000000 | bytes 8388608 | tf_op jit(solution)/shard_map/pallas_call | solution.py:152
  203.9 1.3 collective-permute-start.9
  205.2 11.8 %collective-permute-start.8 = (f32[4,128,32]{2,1,0:T(8,128)S(1)}, f32[4,128,32]{2,1,0:T(8,128)S(1)}, u32[]{:S(2)}, u32[]{:S(2)}) collective-permute-start(f32[4,128,32]{2,1,0:T(8,128)S(1)} %get-tuple-element.39), channel_id=1, source_target_pairs={{0,4},{4,8},{8,12},{1,5},{5,9},{9,13},{2,6},{6,10},{10,14},{3,7},{... | collective-permute-start | bytes 196616 | tf_op jit(solution)/shard_map/ppermute | solution.py:306
  217.0 3.8 %collective-permute-done.9.r_ref = f32[4,128,32]{2,1,0:T(8,128)S(1)} collective-permute-done((f32[4,128,32]{2,1,0:T(8,128)S(1)}, f32[4,128,32]{2,1,0:T(8,128)S(1)}, u32[]{:S(2)}, u32[]{:S(2)}) %collective-permute-start.9) | collective-permute-done | bytes 65568 | tf_op jit(solution)/shard_map/ppermute | solution.py:307
  220.9 1.2 collective-permute-done.8.l_ref
  222.0 3.8 %shard_map.118 = (f32[2,512,1024]{2,1,0:T(8,128)}, f32[8,128]{1,0:T(8,128)S(1)}) custom-call(s32[2,2]{1,0:T(2,128)S(1)} %copy-done, f32[4,128,1024]{2,1,0:T(8,128)S(1)} %shard_map.117.p_ref, f32[4,128,32]{2,1,0:T(8,128)S(1)} %collective-permute-done.8.l_ref, f32[4,128,32]{2,1,0:T(8,128)S(1)} %collective-permute-done.9.r_ref, ...), custom_call_target="tpu_custom_call", output_to_operand_aliasing={{0}: (6, {})} | custom-call | flops 2000000000 | bytes 5242880 | tf_op jit(solution)/shard_map/pallas_call | solution.py:220
  227.1 1.0 collective-permute-start.10
  229.1 2.8 %collective-permute-start.11 = (f32[1]{0:T(128)}, f32[1]{0:T(128)}, u32[]{:S(2)}, u32[]{:S(2)}) collective-permute-start(f32[1]{0:T(128)} %add.77), channel_id=1, source_target_pairs={{0,2},{2,0},{1,3},{3,1},{4,6},{6,4},{5,7},{7,5},{8,10},{10,8},{9,1... | collective-permute-start | bytes 20 | tf_op jit(solution)/shard_map/ppermute | solution.py:245
  231.9 0.9 collective-permute-done.11
  233.5 3.8 %collective-permute-start.12 = (f32[1]{0:T(128)}, f32[1]{0:T(128)}, u32[]{:S(2)}, u32[]{:S(2)}) collective-permute-start(f32[1]{0:T(128)} %add.78), channel_id=1, source_target_pairs={{0,4},{4,0},{8,12},{12,8},{1,5},{5,1},{9,13},{13,9},{2,6},{6,2},{1... | collective-permute-start | bytes 20 | tf_op jit(solution)/shard_map/ppermute | solution.py:245
  238.3 5.3 %collective-permute-start.13 = (f32[1]{0:T(128)}, f32[1]{0:T(128)}, u32[]{:S(2)}, u32[]{:S(2)}) collective-permute-start(f32[1]{0:T(128)} %add.79), channel_id=1, source_target_pairs={{0,8},{4,12},{8,0},{12,4},{1,9},{5,13},{9,1},{13,5},{2,10},{6,14},... | collective-permute-start | bytes 20 | tf_op jit(solution)/shard_map/ppermute | solution.py:245
  (31 shorter events, 3.5 us)
Async XLA Ops:
  14.4 29.0 %collective-permute-start.3 = (f32[2,128,1024]{2,1,0:T(8,128)}, f32[2,128,1024]{2,1,0:T(8,128)S(1)}, u32[]{:S(2)}, u32[]{:S(2)}) collective-permute-start(f32[2,128,1024]{2,1,0:T(8,128)} %get-tuple-element.24), channel_id=1, source_target_pairs={{0,12},{4,0},{8,4},{12,8},{1,13},{5,1},{9,5},{13,9},{2,14},{6,2},{... | collective-permute-start | bytes 3145736 | tf_op jit(solution)/shard_map/ppermute | solution.py:284
  19.5 92.2 %collective-permute-start.4 = (f32[2,128,1024]{2,1,0:T(8,128)}, f32[2,128,1024]{2,1,0:T(8,128)S(1)}, u32[]{:S(2)}, u32[]{:S(2)}) collective-permute-start(f32[2,128,1024]{2,1,0:T(8,128)} %get-tuple-element.25), channel_id=1, source_target_pairs={{0,8},{4,12},{8,0},{12,4},{1,9},{5,13},{9,1},{13,5},{2,10},{6,14},... | collective-permute-start | bytes 3145736 | tf_op jit(solution)/shard_map/ppermute | solution.py:284
  19.5 15.4 %copy-start.5 = (s32[2,2]{1,0:T(2,128)S(1)}, s32[2,2]{1,0:T(2,128)}, u32[]{:S(2)}) copy-start(s32[2,2]{1,0:T(2,128)} %param.12) | copy-start | bytes 52
  19.5 92.2 %collective-permute-start.5 = (f32[2,128,1024]{2,1,0:T(8,128)}, f32[2,128,1024]{2,1,0:T(8,128)S(1)}, u32[]{:S(2)}, u32[]{:S(2)}) collective-permute-start(f32[2,128,1024]{2,1,0:T(8,128)} %get-tuple-element.26), channel_id=1, source_target_pairs={{0,4},{4,8},{8,12},{12,0},{1,5},{5,9},{9,13},{13,1},{2,6},{6,10},{... | collective-permute-start | bytes 3145736 | tf_op jit(solution)/shard_map/ppermute | solution.py:284
  30.9 143.2 %collective-permute-start = (f32[2,128,1024]{2,1,0:T(8,128)}, f32[2,128,1024]{2,1,0:T(8,128)S(1)}, u32[]{:S(2)}, u32[]{:S(2)}) collective-permute-start(f32[2,128,1024]{2,1,0:T(8,128)} %get-tuple-element.20), channel_id=1, source_target_pairs={{0,12},{4,0},{8,4},{12,8},{1,13},{5,1},{9,5},{13,9},{2,14},{6,2},{... | collective-permute-start | bytes 3145736 | tf_op jit(solution)/shard_map/ppermute | solution.py:284
  33.7 166.7 %collective-permute-start.1 = (f32[2,128,1024]{2,1,0:T(8,128)}, f32[2,128,1024]{2,1,0:T(8,128)S(1)}, u32[]{:S(2)}, u32[]{:S(2)}) collective-permute-start(f32[2,128,1024]{2,1,0:T(8,128)} %get-tuple-element.21), channel_id=1, source_target_pairs={{0,8},{4,12},{8,0},{12,4},{1,9},{5,13},{9,1},{13,5},{2,10},{6,14},... | collective-permute-start | bytes 3145736 | tf_op jit(solution)/shard_map/ppermute | solution.py:284
  43.4 157.0 %collective-permute-start.2 = (f32[2,128,1024]{2,1,0:T(8,128)}, f32[2,128,1024]{2,1,0:T(8,128)S(1)}, u32[]{:S(2)}, u32[]{:S(2)}) collective-permute-start(f32[2,128,1024]{2,1,0:T(8,128)} %get-tuple-element.22), channel_id=1, source_target_pairs={{0,4},{4,8},{8,12},{12,0},{1,5},{5,9},{9,13},{13,1},{2,6},{6,10},{... | collective-permute-start | bytes 3145736 | tf_op jit(solution)/shard_map/ppermute | solution.py:284
  111.7 1.4 copy-start.1
  113.1 1.2 copy-start.4
  114.3 56.0 %copy-start = (s32[2,2]{1,0:T(2,128)S(1)}, s32[2,2]{1,0:T(2,128)}, u32[]{:S(2)}) copy-start(s32[2,2]{1,0:T(2,128)} %scale_ref.3) | copy-start | bytes 52
  117.8 51.4 %collective-permute-start.7 = (f32[4,128,32]{2,1,0:T(8,128)S(1)}, f32[4,128,32]{2,1,0:T(8,128)S(1)}, u32[]{:S(2)}, u32[]{:S(2)}) collective-permute-start(f32[4,128,32]{2,1,0:T(8,128)S(1)} %get-tuple-element.40), channel_id=1, source_target_pairs={{4,0},{8,4},{12,8},{5,1},{9,5},{13,9},{6,2},{10,6},{14,10},{7,3},{... | collective-permute-start | bytes 196616 | tf_op jit(solution)/shard_map/ppermute | solution.py:307
  119.1 51.2 %collective-permute-start.6 = (f32[4,128,32]{2,1,0:T(8,128)S(1)}, f32[4,128,32]{2,1,0:T(8,128)S(1)}, u32[]{:S(2)}, u32[]{:S(2)}) collective-permute-start(f32[4,128,32]{2,1,0:T(8,128)S(1)} %get-tuple-element.41), channel_id=1, source_target_pairs={{0,4},{4,8},{8,12},{1,5},{5,9},{9,13},{2,6},{6,10},{10,14},{3,7},{... | collective-permute-start | bytes 196616 | tf_op jit(solution)/shard_map/ppermute | solution.py:306
  166.3 34.2 %copy-start.2 = (bf16[4,256,768]{2,1,0:T(8,128)(2,1)S(1)}, bf16[4,256,768]{2,1,0:T(8,128)(2,1)}, u32[]{:S(2)}) copy-start(bf16[4,256,768]{2,1,0:T(8,128)(2,1)} %constant.50.clone.t_ref) | copy-start | bytes 4718596
  166.3 34.2 %copy-start.3 = (f32[2,128,1024]{2,1,0:T(8,128)S(1)}, f32[2,128,1024]{2,1,0:T(8,128)}, u32[]{:S(2)}) copy-start(f32[2,128,1024]{2,1,0:T(8,128)} %get-tuple-element.28.x0) | copy-start | bytes 3145732
  203.9 17.0 %collective-permute-start.9 = (f32[4,128,32]{2,1,0:T(8,128)S(1)}, f32[4,128,32]{2,1,0:T(8,128)S(1)}, u32[]{:S(2)}, u32[]{:S(2)}) collective-permute-start(f32[4,128,32]{2,1,0:T(8,128)S(1)} %get-tuple-element.38), channel_id=1, source_target_pairs={{4,0},{8,4},{12,8},{5,1},{9,5},{13,9},{6,2},{10,6},{14,10},{7,3},{... | collective-permute-start | bytes 196616 | tf_op jit(solution)/shard_map/ppermute | solution.py:307
  205.2 16.8 %collective-permute-start.8 = (f32[4,128,32]{2,1,0:T(8,128)S(1)}, f32[4,128,32]{2,1,0:T(8,128)S(1)}, u32[]{:S(2)}, u32[]{:S(2)}) collective-permute-start(f32[4,128,32]{2,1,0:T(8,128)S(1)} %get-tuple-element.39), channel_id=1, source_target_pairs={{0,4},{4,8},{8,12},{1,5},{5,9},{9,13},{2,6},{6,10},{10,14},{3,7},{... | collective-permute-start | bytes 196616 | tf_op jit(solution)/shard_map/ppermute | solution.py:306
  227.1 1.4 collective-permute-start.10
  229.1 3.7 %collective-permute-start.11 = (f32[1]{0:T(128)}, f32[1]{0:T(128)}, u32[]{:S(2)}, u32[]{:S(2)}) collective-permute-start(f32[1]{0:T(128)} %add.77), channel_id=1, source_target_pairs={{0,2},{2,0},{1,3},{3,1},{4,6},{6,4},{5,7},{7,5},{8,10},{10,8},{9,1... | collective-permute-start | bytes 20 | tf_op jit(solution)/shard_map/ppermute | solution.py:245
  233.5 4.2 %collective-permute-start.12 = (f32[1]{0:T(128)}, f32[1]{0:T(128)}, u32[]{:S(2)}, u32[]{:S(2)}) collective-permute-start(f32[1]{0:T(128)} %add.78), channel_id=1, source_target_pairs={{0,4},{4,0},{8,12},{12,8},{1,5},{5,1},{9,13},{13,9},{2,6},{6,2},{1... | collective-permute-start | bytes 20 | tf_op jit(solution)/shard_map/ppermute | solution.py:245
  238.3 5.6 %collective-permute-start.13 = (f32[1]{0:T(128)}, f32[1]{0:T(128)}, u32[]{:S(2)}, u32[]{:S(2)}) collective-permute-start(f32[1]{0:T(128)} %add.79), channel_id=1, source_target_pairs={{0,8},{4,12},{8,0},{12,4},{1,9},{5,13},{9,1},{13,5},{2,10},{6,14},... | collective-permute-start | bytes 20 | tf_op jit(solution)/shard_map/ppermute | solution.py:245
